TPU v7x, 32 devices: a whole 2x2x4 slice. The times are simulated.
32 devices in a mesh: img: 4 (over x, core), tp: 8 (over z, y).
Axes of the slice: x: 2, y: 2, z: 4, core: 2. Of those that a mesh axis runs over, the one named last changes fastest.
Arguments:
- patch_tokens: bfloat16 [4096, 1024], P(('img', 'tp')), may hold values from -12 to 12
- norm_gain: float32 [1024], replicated, may hold values from 0.1 to 1.9
- norm_bias: float32 [1024], replicated, may hold values from -3 to 3
- up_weight: bfloat16 [1024, 8192], P('img', 'tp'), may hold values from -0.1875 to 0.1875
- up_bias: float32 [8192], P('tp'), may hold values from -3 to 3
- down_weight: bfloat16 [8192, 4096], P('tp', 'img'), may hold values from -0.125 to 0.125
- down_bias: float32 [4096], replicated, may hold values from -3 to 3
Outputs:
- projected: bfloat16 [4096, 4096], P(('img', 'tp'))
All inputs are finite; a program needn't handle non-finite values.
Results may differ from a plain program's by a relative error of at most 0.014.
Values may be sent and summed in bfloat16 or wider, within the bound.
A program may use at most 128 MiB of HBM per device.

v0:
```python
import functools

import jax
import jax.numpy as jnp
from jax import lax
from jax.experimental import pallas as pl
from jax.experimental.pallas import tpu as pltpu
from jax.sharding import PartitionSpec as P

MESH = pl.DeviceIdType.MESH
LANES = 128
UP_STAGES = 2


def kernel(n_img, n_tp, x_ref, gain_ref, nbias_ref, up_ref, ubias_ref, down_ref, dbias_ref, out_ref,
           tok, normed, upf, ubf, hidden, dn, pb, from_low, from_high, sums,
           tk_s, tk_r, bs_s, bs_r, own_sem, dx_s, dx_r, dm_s, dm_r, r1_s, r1_r, r2_s, r2_r,
           p_s, p_r, lo_s, lo_r, hi_s, hi_r):
    cores = 2 if n_img % 2 == 0 else 1
    pair = 2 if n_tp % 2 == 0 else 1
    n_x, n_g = n_img // cores, n_tp // pair
    img, tp = lax.axis_index("img"), lax.axis_index("tp")
    x, c = img // cores, img % cores
    g, m = tp // pair, tp % pair
    rows, width = x_ref.shape
    depth, units = up_ref.shape
    n_chunk = down_ref.shape[1] // LANES
    u_rows = depth // UP_STAGES
    stages = UP_STAGES + n_chunk

    def at_x(k):
        return {"img": lax.rem(x + k, n_x) * cores + c, "tp": tp}

    def at_m(k):
        return {"img": img, "tp": g * pair + lax.rem(m + k, pair)}

    def at_g(k):
        return {"img": img, "tp": lax.rem(g + k, n_g) * pair + m}

    partner = {"img": x * cores + (cores - 1 - c), "tp": tp}
    xs, ms, gs = range(1, n_x), range(1, pair), range(1, n_g)

    def is_up(s):
        return isinstance(s, int) and s < UP_STAGES

    def source(s):
        if is_up(s):
            return up_ref.at[pl.ds(s * u_rows, u_rows), :]
        return down_ref.at[:, pl.ds(pl.multiple_of((s - UP_STAGES) * LANES, LANES), LANES)]

    def block(s, kx, km, core, half=None):
        src = lax.rem(x - kx + n_x, n_x) * cores + core
        src_m = lax.rem(m - km + pair, pair)
        if is_up(s):
            size, lo = u_rows, src * depth + s * u_rows
            if half is not None:
                size, lo = u_rows // 2, lo + half * (u_rows // 2)
            return upf.at[src_m, pl.ds(pl.multiple_of(lo, size), size), :]
        size, lo = units, src_m * units
        if half is not None:
            size, lo = units // 2, lo + half * (units // 2)
        return dn.at[s - UP_STAGES, pl.ds(pl.multiple_of(lo, size), size),
                     pl.ds(pl.multiple_of(src * LANES, LANES), LANES)]

    def copy(src, dst, send, recv, device):
        return pltpu.make_async_remote_copy(
            src_ref=src, dst_ref=dst, send_sem=send, recv_sem=recv,
            device_id=device, device_id_type=MESH)

    def direct_x(s, k, src, dst):
        return copy(src, dst, dx_s.at[s, k], dx_r.at[s, k], at_x(k))

    def direct_m(s, k, src, dst):
        return copy(src, dst, dm_s.at[s, k], dm_r.at[s, k], at_m(k))

    def relay_m(s, kx, km, ref):
        return copy(ref, ref, r1_s.at[s, kx, km], r1_r.at[s, kx, km], at_m(km))

    def relay_x(s, kx, km, ref):
        return copy(ref, ref, r2_s.at[s, kx, km], r2_r.at[s, kx, km], at_x(kx))

    def across(s, kx, km, src, dst):
        return copy(src, dst, p_s.at[s, kx, km], p_r.at[s, kx, km], partner)

    def own_copy(s):
        return pltpu.make_async_copy(source(s), block(s, 0, 0, c), own_sem.at[s])

    def issue(s):
        here, place = source(s), block(s, 0, 0, c)
        for k in xs:
            direct_x(s, k, here, place).start()
        for k in ms:
            direct_m(s, k, here, place).start()
        if cores > 1:
            across(s, 0, 0, here, place).start()
        own_copy(s).start()

    def forward(s):
        for k in xs:
            ref = block(s, k, 0, c)
            direct_x(s, k, ref, ref).wait_recv()
            for km in ms:
                relay_m(s, k, km, block(s, k, 0, c, 0)).start()
            if cores > 1:
                across(s, k, 0, ref, ref).start()
        for km in ms:
            ref = block(s, 0, km, c)
            direct_m(s, km, ref, ref).wait_recv()
            for k in xs:
                relay_x(s, k, km, block(s, 0, km, c, 1)).start()
            if cores > 1:
                across(s, 0, km, ref, ref).start()

    def collect(s):
        for k in xs:
            for km in ms:
                relay_m(s, k, km, block(s, k, km, c, 0)).wait_recv()
                relay_x(s, k, km, block(s, k, km, c, 1)).wait_recv()
                if cores > 1:
                    ref = block(s, k, km, c)
                    across(s, k, km, ref, ref).start()
        own_copy(s).wait()
        if cores > 1:
            for k in range(n_x):
                for km in range(pair):
                    ref = block(s, k, km, cores - 1 - c)
                    across(s, k, km, ref, ref).wait_recv()

    def finish(s):
        for k in xs:
            direct_x(s, k, source(s), source(s)).wait_send()
        for km in ms:
            direct_m(s, km, source(s), source(s)).wait_send()
        for k in xs:
            for km in ms:
                relay_m(s, k, km, block(s, k, 0, c, 0)).wait_send()
                relay_x(s, k, km, block(s, 0, km, c, 1)).wait_send()
        if cores > 1:
            for k in range(n_x):
                for km in range(pair):
                    ref = block(s, k, km, c)
                    across(s, k, km, ref, ref).wait_send()

    def token(k, src, slot):
        return copy(src, tok.at[slot], tk_s.at[k], tk_r.at[k], at_g(k))

    def bias(k, src, slot):
        return copy(src, ubf.at[slot], bs_s.at[k], bs_r.at[k], at_m(k))

    def upward(j, d):
        return copy(pb.at[j, d], from_low.at[j, d], lo_s.at[j, d], lo_r.at[j, d], at_g(1))

    def downward(j, d):
        return copy(pb.at[j, d], from_high.at[j, d], hi_s.at[j, d], hi_r.at[j, d], at_g(n_g - 1))

    def normalize(values, at):
        values = values.astype(jnp.float32)
        center = jnp.mean(values, axis=1, keepdims=True)
        spread = jnp.mean((values - center) ** 2, axis=1, keepdims=True)
        lines = (values - center) * lax.rsqrt(spread + 1e-05) * gain_ref[...] + nbias_ref[...]
        normed[pl.ds(pl.multiple_of(at * rows, rows), rows), :] = lines.astype(jnp.bfloat16)

    barrier = pltpu.get_barrier_semaphore()
    near = [at_x(k) for k in xs] + [at_m(k) for k in ms] + [at_g(k) for k in gs]
    if cores > 1:
        near.append(partner)
    for device in near:
        pl.semaphore_signal(barrier, inc=1, device_id=device, device_id_type=MESH)
    pl.semaphore_wait(barrier, len(near))

    for k in gs:
        token(k, x_ref, k - 1).start()
    for k in ms:
        bias(k, ubias_ref, k - 1).start()
    issue(0)
    issue(1)
    normalize(x_ref[...], g)

    forward(0)
    issue(2)
    forward(1)
    if stages > 3:
        issue(3)
    collect(0)
    forward(2)
    if stages > 4:
        issue(4)
    for k in gs:
        token(k, x_ref, k - 1).wait_recv()
        normalize(tok[k - 1], lax.rem(g - k + n_g, n_g))
    for k in ms:
        bias(k, ubias_ref, k - 1).wait_recv()
    collect(1)

    tile = 256
    per_m = units // tile

    for km in range(pair):
        place = lax.rem(m - km + pair, pair)
        biases = ubias_ref if km == 0 else ubf.at[km - 1]

        def up_tile(n, carry):
            cols = pl.ds(pl.multiple_of(n * tile, tile), tile)
            summed = jnp.dot(normed[...], upf[place, :, cols], preferred_element_type=jnp.float32)
            wide = pl.ds(pl.multiple_of(place * units + n * tile, tile), tile)
            hidden[:, wide] = jax.nn.gelu(summed + biases[:, cols]).astype(jnp.bfloat16)
            return carry

        lax.fori_loop(0, per_m, up_tile, 0)

    def multiply(j):
        def down_tile(n, carry):
            cols = pl.ds(pl.multiple_of(n * tile, tile), tile)
            value = jnp.dot(hidden[...], dn[j, :, cols], preferred_element_type=jnp.float32)
            pb[j, :, :, cols] = value.reshape(n_g, rows, tile).astype(jnp.bfloat16)
            return carry

        lax.fori_loop(0, n_img * LANES // tile, down_tile, 0)

    def pass_on(step):
        j_up, j_down = step - g, step - (n_g - 1 - g)
        go_up = (g < n_g - 1) & (j_up >= 0) & (j_up < n_chunk)
        go_down = (g > 0) & (j_down >= 0) & (j_down < n_chunk)

        def accumulate(j, d, copies, arrived):
            copies(j, d).wait_recv()
            pb[j, d] = (pb[j, d].astype(jnp.float32) + arrived[j, d].astype(jnp.float32)).astype(jnp.bfloat16)

        for k in range(n_g - 1):
            high, low = n_g - 1 - k, k

            @pl.when(go_up & (g > 0) & (g < high))
            def _():
                accumulate(j_up, high, upward, from_low)

            @pl.when(go_down & (g < n_g - 1) & (g > low))
            def _():
                accumulate(j_down, low, downward, from_high)

            @pl.when(go_up & (g < high))
            def _():
                upward(j_up, high).start()

            @pl.when(go_down & (g > low))
            def _():
                downward(j_down, low).start()

    def tick(s, carry):
        @pl.when(s < stages)
        def _():
            forward(s)

        @pl.when(s + 2 < stages)
        def _():
            issue(s + 2)

        step = s - 1 - UP_STAGES
        collect(s - 1)
        multiply(step)
        pass_on(step)

        @pl.when(step >= n_g)
        def _():
            reduce(step - n_g)
        return carry

    def reduce(j):
        total = pb[j, g].astype(jnp.float32)
        for i in range(n_img):
            cols = pl.ds(pl.multiple_of((i * n_chunk + j) * LANES, LANES), LANES)
            piece = slice(i * LANES, (i + 1) * LANES)
            sums[:, piece] = total[:, piece] + dbias_ref[:, cols]
        for first, copies, arrived in ((g > 0, upward, from_low), (g < n_g - 1, downward, from_high)):
            @pl.when(first)
            def _():
                copies(j, g).wait_recv()
                sums[...] += arrived[j, g].astype(jnp.float32)
        for i in range(n_img):
            cols = pl.ds(pl.multiple_of((i * n_chunk + j) * LANES, LANES), LANES)
            out_ref[:, cols] = sums[:, i * LANES:(i + 1) * LANES].astype(jnp.bfloat16)

    def drain(step, carry):
        pass_on(step)
        return carry

    def reduce_tick(j, carry):
        reduce(j)
        return carry

    def sent(j, carry):
        for d in range(n_g):
            @pl.when(g < d)
            def _():
                upward(j, d).wait_send()

            @pl.when(g > d)
            def _():
                downward(j, d).wait_send()
        return carry

    lax.fori_loop(UP_STAGES + 1, stages + 1, tick, 0)
    lax.fori_loop(n_chunk, n_chunk + n_g - 2, drain, 0)
    lax.fori_loop(max(n_chunk - n_g, 0), n_chunk, reduce_tick, 0)
    lax.fori_loop(0, n_chunk, sent, 0)
    for s in range(UP_STAGES):
        finish(s)

    def finish_tick(s, carry):
        finish(s)
        return carry

    lax.fori_loop(UP_STAGES, stages, finish_tick, 0)
    for k in gs:
        token(k, x_ref, k - 1).wait_send()
    for k in ms:
        bias(k, ubias_ref, k - 1).wait_send()


def solution(mesh):
    n_img, n_tp = mesh.shape["img"], mesh.shape["tp"]
    cores = 2 if n_img % 2 == 0 else 1
    pair = 2 if n_tp % 2 == 0 else 1
    n_x, n_g = n_img // cores, n_tp // pair

    def on_device(x, gain, nbias, up, ubias, down, dbias):
        rows, width = x.shape
        depth, units = up.shape
        n_chunk = down.shape[1] // LANES
        stages = UP_STAGES + n_chunk
        wide = n_img * LANES
        bf16 = jnp.bfloat16
        dma = pltpu.SemaphoreType.DMA
        scratch = [
            pltpu.VMEM((max(n_g - 1, 1), rows, width), bf16),
            pltpu.VMEM((n_g * rows, width), bf16),
            pltpu.VMEM((pair, width, units), bf16),
            pltpu.VMEM((max(pair - 1, 1), 1, units), jnp.float32),
            pltpu.VMEM((n_g * rows, pair * units), bf16),
            pltpu.VMEM((n_chunk, pair * units, wide), bf16),
            pltpu.VMEM((n_chunk, n_g, rows, wide), bf16),
            pltpu.VMEM((n_chunk, n_g, rows, wide), bf16),
            pltpu.VMEM((n_chunk, n_g, rows, wide), bf16),
            pltpu.VMEM((rows, wide), jnp.float32),
        ]
        scratch += [dma((n_g,))] * 2 + [dma((pair,))] * 2 + [dma((stages,))]
        scratch += [dma((stages, n_x))] * 2 + [dma((stages, pair))] * 2
        scratch += [dma((stages, n_x, pair))] * 6 + [dma((n_chunk, n_g))] * 4
        return pl.pallas_call(
            functools.partial(kernel, n_img, n_tp),
            out_shape=jax.ShapeDtypeStruct((rows, n_img * down.shape[1]), bf16),
            in_specs=[pl.BlockSpec(memory_space=pltpu.VMEM)] * 7,
            out_specs=pl.BlockSpec(memory_space=pltpu.VMEM),
            scratch_shapes=scratch,
            compiler_params=pltpu.CompilerParams(
                collective_id=0, has_side_effects=True, vmem_limit_bytes=60 * 1024 * 1024),
        )(x, gain.reshape(1, -1), nbias.reshape(1, -1), up, ubias.reshape(1, -1), down,
          dbias.reshape(1, -1))

    return jax.shard_map(
        on_device,
        mesh=mesh,
        in_specs=(P(("img", "tp"), None), P(), P(), P("img", "tp"), P("tp"), P("tp", "img"), P()),
        out_specs=P(("img", "tp"), None),
        check_vma=False,
    )
```

profile of v0, /device:TPU:0, one launch (start us, length us, event | category | flops | bytes accessed | tf_op | source)
XLA Modules:
  0.0 122.5 jit_solution(3807968154897473095)
XLA Ops:
  0.0 120.2 %shard_map.73 = bf16[128,4096]{1,0:T(8,128)(2,1)} custom-call(bf16[128,1024]{1,0:T(8,128)(2,1)} %x_ref.1, f32[1,1024]{1,0:T(1,128)} %bitcast.5, f32[1,1024]{1,0:T(1,128)} %bitcast.6, bf16[256,1024]{1,0:T(8,128)(2,1)} %up_ref.1, f32[1,1024]{1,0:T(1,128)} %bitcast.7, bf16[1024,1024]{1,0:T(8,128)(2,1)} %down_ref.1, f32[1,4096]{1,0:T(1,128)} %bitcast.4), custom_call_target="tpu_custom_call" | custom-call | tf_op jit(solution)/shard_map/pallas_call | solution.py:348
  120.2 2.3 %copy.9 = bf16[128,4096]{1,0:T(8,128)(2,1)} copy(bf16[128,4096]{1,0:T(8,128)(2,1)} %shard_map.73) | data formatting | bytes 2097152
where the time goes:
time: 123 us; the launch traced here: 122 us
  Pallas kernels  120 us (98%)
  local copies, waits for them, and re-layouts  2.29 us (2%)
    pallas_call x1, Pallas kernels, on_device(): pl.pallas_call(functools.partial(kernel, n_img, n_tp), out_shape=jax.Shap...  120 us

commit v1 on v0

v1 whole, which is shorter than its diff:
```python
import functools

import jax
import jax.numpy as jnp
from jax import lax
from jax.experimental import pallas as pl
from jax.experimental.pallas import tpu as pltpu
from jax.sharding import PartitionSpec as P

MESH = pl.DeviceIdType.MESH
LANES = 128
UP_STAGES = 2
LAG = 2
TILE = 256


def portion(size, num, den):
    return max(size * num // den // 16 * 16, 16)


def kernel(n_img, n_tp, x_hbm, gain_hbm, nbias_hbm, up_hbm, ubias_hbm, down_hbm, dbias_hbm, out_hbm,
           xv, gain, nbias, ubias, dbias, tok, normed, upf, ubf, hidden, dn, pb, from_low, from_high, ov,
           in_sem, own_sem, out_sem, tu_s, tu_r, td_s, td_r, bs_s, bs_r,
           dx_s, dx_r, dm_s, dm_r, r1_s, r1_r, r2_s, r2_r, p_s, p_r, lo_s, lo_r, hi_s, hi_r):
    cores = 2 if n_img % 2 == 0 else 1
    pair = 2 if n_tp % 2 == 0 else 1
    n_x, n_g = n_img // cores, n_tp // pair
    img, tp = lax.axis_index("img"), lax.axis_index("tp")
    x, c = img // cores, img % cores
    g, m = tp // pair, tp % pair
    rows, width = xv.shape
    depth, units = up_hbm.shape
    n_chunk = down_hbm.shape[1] // LANES
    u_rows = depth // UP_STAGES
    stages = UP_STAGES + n_chunk
    wide = cores * LANES
    n_v = n_chunk * n_x
    xs, ms, hops = range(1, n_x), range(1, pair), range(1, n_g)
    low_part = portion(u_rows, 1, 4), portion(units, 9, 16)

    def at_x(k):
        return {"img": lax.rem(x + k, n_x) * cores + c, "tp": tp}

    def at_m(k):
        return {"img": img, "tp": g * pair + lax.rem(m + k, pair)}

    def at_g(k):
        return {"img": img, "tp": lax.rem(g + k, n_g) * pair + m}

    partner = {"img": x * cores + (cores - 1 - c), "tp": tp}

    def is_up(s):
        return isinstance(s, int) and s < UP_STAGES

    def kind(s):
        return 0 if is_up(s) else 1

    def x_from(k):
        return lax.rem(x - k + n_x, n_x)

    def block(s, kx, km, core, part=None):
        src_x = x_from(kx)
        src_m = lax.rem(m - km + pair, pair)
        size = u_rows if is_up(s) else units
        cut = low_part[kind(s)]
        off, size = {None: (0, size), 0: (0, cut), 1: (cut, size - cut)}[part]
        if is_up(s):
            lo = (src_x * cores + core) * depth + s * u_rows + off
            return upf.at[src_m, pl.ds(pl.multiple_of(lo, 16), size), :]
        lo = src_m * units + off
        return dn.at[(s - UP_STAGES) * n_x + src_x, pl.ds(pl.multiple_of(lo, 16), size),
                     pl.ds(pl.multiple_of(core * LANES, LANES), LANES)]

    def copy(src, dst, send, recv, device):
        return pltpu.make_async_remote_copy(
            src_ref=src, dst_ref=dst, send_sem=send, recv_sem=recv,
            device_id=device, device_id_type=MESH)

    def direct_x(s, k, ref):
        return copy(ref, ref, dx_s.at[kind(s), k - 1], dx_r.at[s, k - 1], at_x(k))

    def direct_m(s, k, ref):
        return copy(ref, ref, dm_s.at[kind(s), k - 1], dm_r.at[s, k - 1], at_m(k))

    def relay_m(s, kx, km, ref):
        return copy(ref, ref, r1_s.at[kind(s), kx - 1, km - 1], r1_r.at[s, kx - 1, km - 1], at_m(km))

    def relay_x(s, kx, km, ref):
        return copy(ref, ref, r2_s.at[kind(s), kx - 1, km - 1], r2_r.at[s, kx - 1, km - 1], at_x(kx))

    def across(s, kx, km, ref):
        return copy(ref, ref, p_s.at[kind(s)], p_r.at[s, km if is_up(s) else kx], partner)

    def issue(s):
        ref = block(s, 0, 0, c)
        for k in ms:
            direct_m(s, k, ref).start()
        for k in xs:
            direct_x(s, k, ref).start()
        if cores > 1:
            across(s, 0, 0, ref).start()

    def forward(s):
        for km in ms:
            ref = block(s, 0, km, c)
            direct_m(s, km, ref).wait_recv()
            if cores > 1:
                across(s, 0, km, ref).start()
            for k in xs:
                relay_x(s, k, km, block(s, 0, km, c, 1)).start()
        for k in xs:
            ref = block(s, k, 0, c)
            direct_x(s, k, ref).wait_recv()
            for km in ms:
                relay_m(s, k, km, block(s, k, 0, c, 0)).start()
            if cores > 1:
                across(s, k, 0, ref).start()

    def collect(s, k):
        for km in ms:
            relay_m(s, k, km, block(s, k, km, c, 0)).wait_recv()
            relay_x(s, k, km, block(s, k, km, c, 1)).wait_recv()
            if cores > 1:
                across(s, k, km, block(s, k, km, c)).start()

    def take_up(s, km):
        if cores > 1:
            ref = upf.at[0, pl.ds(0, n_x * u_rows), :]
            across(s, 0, km, ref).wait_recv()

    def take(s, k):
        if cores > 1:
            ref = dn.at[(s - UP_STAGES) * n_x + x_from(k), :,
                        pl.ds(pl.multiple_of((cores - 1 - c) * LANES, LANES), LANES)]
            across(s, k, 0, ref).wait_recv()

    def own_down(j):
        return pltpu.make_async_copy(
            down_hbm.at[:, pl.ds(pl.multiple_of(j * LANES, LANES), LANES)],
            block(j + UP_STAGES, 0, 0, c), own_sem.at[j])

    def half(ref, h):
        return ref.at[pl.ds(h * (rows // 2), rows // 2), :]

    def token_up(e, h):
        src = xv if e == 0 else tok.at[g - e]
        return copy(half(src, h), half(tok.at[g - e], h), tu_s.at[e], tu_r.at[e, h], at_g(1))

    def token_down(e, h):
        src = xv if e == 0 else tok.at[g + e]
        return copy(half(src, h), half(tok.at[g + e], h), td_s.at[e], td_r.at[e, h], at_g(n_g - 1))

    def token_start(e):
        for h in range(2):
            @pl.when((g >= e) & (g < n_g - 1))
            def _():
                if e > 0:
                    ref = half(tok.at[g - e], h)
                    copy(ref, ref, tu_s.at[e], tu_r.at[e - 1, h], at_g(1)).wait_recv()
                token_up(e, h).start()

            @pl.when((g <= n_g - 1 - e) & (g > 0))
            def _():
                if e > 0:
                    ref = half(tok.at[g + e], h)
                    copy(ref, ref, td_s.at[e], td_r.at[e - 1, h], at_g(n_g - 1)).wait_recv()
                token_down(e, h).start()

    def token_end():
        for e in hops:
            for h in range(2):
                @pl.when((g >= e) & (g == n_g - 1))
                def _():
                    ref = half(tok.at[g - e], h)
                    copy(ref, ref, tu_s.at[0], tu_r.at[e - 1, h], at_g(1)).wait_recv()

                @pl.when((g <= n_g - 1 - e) & (g == 0))
                def _():
                    ref = half(tok.at[g + e], h)
                    copy(ref, ref, td_s.at[0], td_r.at[e - 1, h], at_g(n_g - 1)).wait_recv()

    def bias(k, src, slot):
        return copy(src, ubf.at[slot], bs_s.at[slot], bs_r.at[slot], at_m(k))

    def upward(v, d):
        return copy(pb.at[v, d], from_low.at[v, d], lo_s.at[d - 1], lo_r.at[v, d - 1], at_g(1))

    def downward(v, d):
        return copy(pb.at[v, d], from_high.at[v, d], hi_s.at[d], hi_r.at[v, d], at_g(n_g - 1))

    def normalize(values, at):
        values = values.astype(jnp.float32)
        center = jnp.mean(values, axis=1, keepdims=True)
        spread = jnp.mean((values - center) ** 2, axis=1, keepdims=True)
        lines = (values - center) * lax.rsqrt(spread + 1e-05) * gain[...] + nbias[...]
        normed[pl.ds(pl.multiple_of(at * rows, rows), rows), :] = lines.astype(jnp.bfloat16)

    barrier = pltpu.get_barrier_semaphore()
    near = [at_x(k) for k in xs] + [at_m(k) for k in ms]
    if cores > 1:
        near.append(partner)

    def greet(device):
        pl.semaphore_signal(barrier, inc=1, device_id=device, device_id_type=MESH)

    for device in near:
        greet(device)

    @pl.when(g < n_g - 1)
    def _():
        greet(at_g(1))

    @pl.when(g > 0)
    def _():
        greet(at_g(n_g - 1))

    own_up = upf.at[m, pl.ds(pl.multiple_of(img * depth, depth), depth), :]
    loads = [pltpu.make_async_copy(a, b, in_sem.at[i]) for i, (a, b) in enumerate((
        (x_hbm, xv), (up_hbm, own_up), (gain_hbm, gain), (nbias_hbm, nbias), (ubias_hbm, ubias), (dbias_hbm, dbias)))]
    for load in loads:
        load.start()
    for j in range(n_chunk):
        own_down(j).start()
    for i in (0, 2, 3, 4, 1):
        loads[i].wait()
    normalize(xv[...], g)

    ends = (g + n_g - 1) // n_g + (2 * n_g - 2 - g) // n_g
    pl.semaphore_wait(barrier, len(near) + ends)

    for s in range(UP_STAGES):
        issue(s)
    if n_g > 1:
        token_start(0)
    for k in ms:
        bias(k, ubias, k - 1).start()
    loads[5].wait()

    def up_rows(km):
        place = lax.rem(m - km + pair, pair)
        biases = ubias if km == 0 else ubf.at[km - 1]

        def up_tile(n, carry):
            cols = pl.ds(pl.multiple_of(n * TILE, TILE), TILE)
            summed = jnp.dot(normed[...], upf[place, :, cols], preferred_element_type=jnp.float32)
            at = pl.ds(pl.multiple_of(place * units + n * TILE, TILE), TILE)
            hidden[:, at] = jax.nn.gelu(summed + biases[:, cols]).astype(jnp.bfloat16)
            return carry

        lax.fori_loop(0, units // TILE, up_tile, 0)

    for s in range(max(UP_STAGES, n_g - 1)):
        if 0 < s + 1 < n_g - 1:
            token_start(s + 1)
        if s < UP_STAGES:
            forward(s)
    for j in range(min(2, n_chunk)):
        own_down(j).wait()
        issue(UP_STAGES + j)
    token_end()
    for k in hops:
        o = lax.rem(g + k, n_g)
        normalize(tok[o], o)
    for s in range(UP_STAGES):
        take_up(s, 0)
    up_rows(0)
    for s in range(UP_STAGES):
        for k in xs:
            collect(s, k)
    for km in ms:
        bias(km, ubias, km - 1).wait_recv()
        for s in range(UP_STAGES):
            take_up(s, km)
        up_rows(km)

    def multiply(v, j, k):
        value = jnp.dot(hidden[...], dn[j * n_x + x_from(k)], preferred_element_type=jnp.float32)
        pb[v] = value.reshape(n_g, rows, wide).astype(jnp.bfloat16)

    def pass_on(step):
        v_up, v_down = step - LAG * g, step - LAG * (n_g - 1 - g)
        go_up = (g < n_g - 1) & (v_up >= 0) & (v_up < n_v)
        go_down = (g > 0) & (v_down >= 0) & (v_down < n_v)

        def accumulate(v, d, copies, arrived):
            copies(v, d).wait_recv()
            pb[v, d] = (pb[v, d].astype(jnp.float32) + arrived[v, d].astype(jnp.float32)).astype(jnp.bfloat16)

        for k in range(n_g - 1):
            high, low = n_g - 1 - k, k

            @pl.when(go_up & (g > 0) & (g < high))
            def _():
                accumulate(v_up, high, upward, from_low)

            @pl.when(go_down & (g < n_g - 1) & (g > low))
            def _():
                accumulate(v_down, low, downward, from_high)

            @pl.when(go_up & (g < high))
            def _():
                upward(v_up, high).start()

            @pl.when(go_down & (g > low))
            def _():
                downward(v_down, low).start()

    def out_copy(cols):
        return pltpu.make_async_copy(ov.at[:, cols], out_hbm.at[:, cols], out_sem.at[0])

    def reduce(v):
        some = (v + n_v - 1) // n_v
        i = (v + n_x - 1) // n_x
        k = lax.rem(v + n_x - 1, n_x) * some + i // n_chunk
        j = i - (k + n_x - 1) // n_x

        @pl.when(g > 0)
        def _():
            upward(v, g).wait_recv()

        @pl.when(g < n_g - 1)
        def _():
            downward(v, g).wait_recv()

        src_x = x_from(k)
        for core in range(cores):
            cols = pl.ds(pl.multiple_of(((src_x * cores + core) * n_chunk + j) * LANES, LANES), LANES)
            piece = slice(core * LANES, (core + 1) * LANES)
            total = pb[v, g, :, piece].astype(jnp.float32) + dbias[:, cols]
            below = from_low[v, g, :, piece].astype(jnp.float32)
            above = from_high[v, g, :, piece].astype(jnp.float32)
            total = total + jnp.where(g > 0, below, 0.0) + jnp.where(g < n_g - 1, above, 0.0)
            ov[:, cols] = total.astype(jnp.bfloat16)
            out_copy(cols).start()

    settle = LAG * (n_g - 1) + 1

    def unit(v, j, k):
        take(j + UP_STAGES, k)
        multiply(v, j, k)
        pass_on(v)

        @pl.when(v >= settle)
        def _():
            reduce(v - settle)

    def later(i, base, first):
        def one(k, carry):
            collect(i + UP_STAGES, k)
            unit(base + k, i, k)
            return carry

        lax.fori_loop(1, n_x, one, 0)

    def tick(i, carry):
        forward(i + UP_STAGES)

        @pl.when(i + 2 < n_chunk)
        def _():
            own_down(i + 2).wait()
            issue(i + 2 + UP_STAGES)

        unit(n_x * (i - 1) + 1, i, 0)
        later(i - 1, n_x * (i - 1) + 1, True)
        return carry

    forward(UP_STAGES)
    if n_chunk > 2:
        own_down(2).wait()
        issue(2 + UP_STAGES)
    unit(0, 0, 0)
    lax.fori_loop(1, n_chunk, tick, 0)
    later(n_chunk - 1, n_x * (n_chunk - 1), False)

    def drain(step, carry):
        pass_on(step)
        return carry

    def reduce_tick(v, carry):
        reduce(v)
        return carry

    lax.fori_loop(n_v, n_v + LAG * (n_g - 2), drain, 0)
    lax.fori_loop(max(n_v - settle, 0), n_v, reduce_tick, 0)

    for t in range(2):
        s = 0 if t == 0 else UP_STAGES
        cut = low_part[t]

        def span(size):
            if t == 0:
                return upf.at[0, pl.ds(0, UP_STAGES * size), :]
            return dn.at[pl.ds(0, n_chunk), pl.ds(0, size), pl.ds(0, LANES)]

        full = u_rows if t == 0 else units
        for k in xs:
            direct_x(s, k, span(full)).wait_send()
        for k in ms:
            direct_m(s, k, span(full)).wait_send()
        for k in xs:
            for km in ms:
                relay_m(s, k, km, span(cut)).wait_send()
                relay_x(s, k, km, span(full - cut)).wait_send()
        if cores > 1:
            ref = upf.at[:, pl.ds(0, n_x * depth), :] if t == 0 else dn.at[:, :, pl.ds(0, LANES)]
            across(s, 0, 0, ref).wait_send()
    for d in range(n_g):
        @pl.when(g < d)
        def _():
            ref = pb.at[:, d]
            copy(ref, ref, lo_s.at[d - 1], lo_r.at[0, 0], at_g(1)).wait_send()

        @pl.when(g > d)
        def _():
            ref = pb.at[:, d]
            copy(ref, ref, hi_s.at[d], hi_r.at[0, 0], at_g(n_g - 1)).wait_send()
    for e in range(n_g - 1):
        @pl.when((g >= e) & (g < n_g - 1))
        def _():
            copy(tok.at[0], tok.at[0], tu_s.at[e], tu_r.at[e, 0], at_g(1)).wait_send()

        @pl.when((g <= n_g - 1 - e) & (g > 0))
        def _():
            copy(tok.at[0], tok.at[0], td_s.at[e], td_r.at[e, 0], at_g(n_g - 1)).wait_send()
    for k in ms:
        bias(k, ubias, k - 1).wait_send()
    pltpu.make_async_copy(ov, out_hbm, out_sem.at[0]).wait()


def solution(mesh):
    n_img, n_tp = mesh.shape["img"], mesh.shape["tp"]
    cores = 2 if n_img % 2 == 0 else 1
    pair = 2 if n_tp % 2 == 0 else 1
    n_x, n_g = n_img // cores, n_tp // pair

    def on_device(x, gain, nbias, up, ubias, down, dbias):
        rows, width = x.shape
        depth, units = up.shape
        n_chunk = down.shape[1] // LANES
        stages = UP_STAGES + n_chunk
        n_v, wide = n_chunk * n_x, cores * LANES
        out_width = n_img * down.shape[1]
        bf16, f32 = jnp.bfloat16, jnp.float32
        dma = pltpu.SemaphoreType.DMA
        ox, om, og = max(n_x - 1, 1), max(pair - 1, 1), max(n_g - 1, 1)
        scratch = [
            pltpu.VMEM((rows, width), bf16),
            pltpu.VMEM((1, width), f32),
            pltpu.VMEM((1, width), f32),
            pltpu.VMEM((1, units), f32),
            pltpu.VMEM((1, out_width), f32),
            pltpu.VMEM((n_g, rows, width), bf16),
            pltpu.VMEM((n_g * rows, width), bf16),
            pltpu.VMEM((pair, width, units), bf16),
            pltpu.VMEM((om, 1, units), f32),
            pltpu.VMEM((n_g * rows, pair * units), bf16),
            pltpu.VMEM((n_v, pair * units, wide), bf16),
            pltpu.VMEM((n_v, n_g, rows, wide), bf16),
            pltpu.VMEM((n_v, n_g, rows, wide), bf16),
            pltpu.VMEM((n_v, n_g, rows, wide), bf16),
            pltpu.VMEM((rows, out_width), bf16),
        ]
        scratch += [dma((6,)), dma((n_chunk,)), dma((1,))]
        scratch += [dma((og,)), dma((og, 2))] * 2 + [dma((om,))] * 2
        scratch += [dma((2, ox)), dma((stages, ox)), dma((2, om)), dma((stages, om))]
        scratch += [dma((2, ox, om)), dma((stages, ox, om))] * 2
        scratch += [dma((2,)), dma((stages, max(n_x, pair)))]
        scratch += [dma((og,)), dma((n_v, og))] * 2
        return pl.pallas_call(
            functools.partial(kernel, n_img, n_tp),
            out_shape=jax.ShapeDtypeStruct((rows, out_width), bf16),
            in_specs=[pl.BlockSpec(memory_space=pl.ANY)] * 7,
            out_specs=pl.BlockSpec(memory_space=pl.ANY),
            scratch_shapes=scratch,
            compiler_params=pltpu.CompilerParams(
                collective_id=0, has_side_effects=True, vmem_limit_bytes=60 * 1024 * 1024),
        )(x, gain.reshape(1, -1), nbias.reshape(1, -1), up, ubias.reshape(1, -1), down,
          dbias.reshape(1, -1))

    return jax.shard_map(
        on_device,
        mesh=mesh,
        in_specs=(P(("img", "tp"), None), P(), P(), P("img", "tp"), P("tp"), P("tp", "img"), P()),
        out_specs=P(("img", "tp"), None),
        check_vma=False,
    )
```

time: 123 us -> 114 us (0.927)
  Pallas kernels: 120 us -> 111 us
    pallas_call x1, Pallas kernels: 120 us -> 111 us  [on_device(): pl.pallas_call(functools.partial(kernel, n_img, n_tp), out_shape=jax.Shap...]
where the time goes in v1:
time: 114 us
  Pallas kernels  111 us (97%)
  local copies, waits for them, and re-layouts  2.29 us (2%)
    pallas_call x1, Pallas kernels, on_device(): pl.pallas_call(functools.partial(kernel, n_img, n_tp), out_shape=jax.Shap...  111 us
    unnamed x1, local copies, waits for them, and re-layouts  2.29 us

profile of v1, /device:TPU:0, one launch (start us, length us, event | category | flops | bytes accessed | tf_op | source)
XLA Modules:
  0.0 113.7 jit_solution(14310316301537475392)
XLA Ops:
  0.0 111.4 %shard_map.73 = bf16[128,4096]{1,0:T(8,128)(2,1)} custom-call(bf16[128,1024]{1,0:T(8,128)(2,1)} %x_hbm.1, f32[1,1024]{1,0:T(1,128)} %bitcast.5, f32[1,1024]{1,0:T(1,128)} %bitcast.6, bf16[256,1024]{1,0:T(8,128)(2,1)} %up_hbm.1, f32[1,1024]{1,0:T(1,128)} %bitcast.7, bf16[1024,1024]{1,0:T(8,128)(2,1)} %down_hbm.1, f32[1,4096]{1,0:T(1,128)} %bitcast.4), custom_call_target="tpu_custom_call" | custom-call | tf_op jit(solution)/shard_map/pallas_call | solution.py:469
  111.4 2.3 %copy.9 = bf16[128,4096]{1,0:T(8,128)(2,1)} copy(bf16[128,4096]{1,0:T(8,128)(2,1)} %shard_map.73) | data formatting | bytes 2097152

commit v2 on v1

--- a/solution.py
+++ b/solution.py
@@ -18,9 +18,9 @@
     return max(size * num // den // 16 * 16, 16)
 
 
-def kernel(n_img, n_tp, x_hbm, gain_hbm, nbias_hbm, up_hbm, ubias_hbm, down_hbm, dbias_hbm, out_hbm,
-           xv, gain, nbias, ubias, dbias, tok, normed, upf, ubf, hidden, dn, pb, from_low, from_high, ov,
-           in_sem, own_sem, out_sem, tu_s, tu_r, td_s, td_r, bs_s, bs_r,
+def kernel(n_img, n_tp, x_hbm, gain_hbm, nbias_hbm, up_hbm, ubias_hbm, down_hbm, dbias_hbm, out_ref,
+           xv, gain, nbias, ubias, dbias, tok, normed, upf, ubf, hidden, dn, pb, from_low, from_high,
+           in_sem, own_sem, tu_s, tu_r, td_s, td_r, bs_s, bs_r,
            dx_s, dx_r, dm_s, dm_r, r1_s, r1_r, r2_s, r2_r, p_s, p_r, lo_s, lo_r, hi_s, hi_r):
     cores = 2 if n_img % 2 == 0 else 1
     pair = 2 if n_tp % 2 == 0 else 1
@@ -36,7 +36,7 @@
     wide = cores * LANES
     n_v = n_chunk * n_x
     xs, ms, hops = range(1, n_x), range(1, pair), range(1, n_g)
-    low_part = portion(u_rows, 1, 4), portion(units, 9, 16)
+    low_part = portion(u_rows, 3, 8), portion(units, 17, 32)
 
     def at_x(k):
         return {"img": lax.rem(x + k, n_x) * cores + c, "tp": tp}
@@ -100,7 +100,7 @@
         if cores > 1:
             across(s, 0, 0, ref).start()
 
-    def forward(s):
+    def forward_m(s):
         for km in ms:
             ref = block(s, 0, km, c)
             direct_m(s, km, ref).wait_recv()
@@ -108,6 +108,8 @@
                 across(s, 0, km, ref).start()
             for k in xs:
                 relay_x(s, k, km, block(s, 0, km, c, 1)).start()
+
+    def forward_x(s):
         for k in xs:
             ref = block(s, k, 0, c)
             direct_x(s, k, ref).wait_recv()
@@ -253,7 +255,8 @@
         if 0 < s + 1 < n_g - 1:
             token_start(s + 1)
         if s < UP_STAGES:
-            forward(s)
+            forward_m(s)
+            forward_x(s)
     for j in range(min(2, n_chunk)):
         own_down(j).wait()
         issue(UP_STAGES + j)
@@ -305,9 +308,6 @@
             def _():
                 downward(v_down, low).start()
 
-    def out_copy(cols):
-        return pltpu.make_async_copy(ov.at[:, cols], out_hbm.at[:, cols], out_sem.at[0])
-
     def reduce(v):
         some = (v + n_v - 1) // n_v
         i = (v + n_x - 1) // n_x
@@ -330,8 +330,7 @@
             below = from_low[v, g, :, piece].astype(jnp.float32)
             above = from_high[v, g, :, piece].astype(jnp.float32)
             total = total + jnp.where(g > 0, below, 0.0) + jnp.where(g < n_g - 1, above, 0.0)
-            ov[:, cols] = total.astype(jnp.bfloat16)
-            out_copy(cols).start()
+            out_ref[:, cols] = total.astype(jnp.bfloat16)
 
     settle = LAG * (n_g - 1) + 1
 
@@ -344,7 +343,7 @@
         def _():
             reduce(v - settle)
 
-    def later(i, base, first):
+    def later(i, base):
         def one(k, carry):
             collect(i + UP_STAGES, k)
             unit(base + k, i, k)
@@ -352,25 +351,26 @@
 
         lax.fori_loop(1, n_x, one, 0)
 
-    def tick(i, carry):
-        forward(i + UP_STAGES)
-
+    def start(i):
         @pl.when(i + 2 < n_chunk)
         def _():
             own_down(i + 2).wait()
             issue(i + 2 + UP_STAGES)
 
+    def tick(i, carry):
+        forward_m(i + UP_STAGES)
         unit(n_x * (i - 1) + 1, i, 0)
-        later(i - 1, n_x * (i - 1) + 1, True)
+        forward_x(i + UP_STAGES)
+        start(i)
+        later(i - 1, n_x * (i - 1) + 1)
         return carry
 
-    forward(UP_STAGES)
-    if n_chunk > 2:
-        own_down(2).wait()
-        issue(2 + UP_STAGES)
+    forward_m(UP_STAGES)
     unit(0, 0, 0)
+    forward_x(UP_STAGES)
+    start(0)
     lax.fori_loop(1, n_chunk, tick, 0)
-    later(n_chunk - 1, n_x * (n_chunk - 1), False)
+    later(n_chunk - 1, n_x * (n_chunk - 1))
 
     def drain(step, carry):
         pass_on(step)
@@ -424,7 +424,6 @@
             copy(tok.at[0], tok.at[0], td_s.at[e], td_r.at[e, 0], at_g(n_g - 1)).wait_send()
     for k in ms:
         bias(k, ubias, k - 1).wait_send()
-    pltpu.make_async_copy(ov, out_hbm, out_sem.at[0]).wait()
 
 
 def solution(mesh):
@@ -458,9 +457,8 @@
             pltpu.VMEM((n_v, n_g, rows, wide), bf16),
             pltpu.VMEM((n_v, n_g, rows, wide), bf16),
             pltpu.VMEM((n_v, n_g, rows, wide), bf16),
-            pltpu.VMEM((rows, out_width), bf16),
         ]
-        scratch += [dma((6,)), dma((n_chunk,)), dma((1,))]
+        scratch += [dma((6,)), dma((n_chunk,))]
         scratch += [dma((og,)), dma((og, 2))] * 2 + [dma((om,))] * 2
         scratch += [dma((2, ox)), dma((stages, ox)), dma((2, om)), dma((stages, om))]
         scratch += [dma((2, ox, om)), dma((stages, ox, om))] * 2
@@ -468,9 +466,9 @@
         scratch += [dma((og,)), dma((n_v, og))] * 2
         return pl.pallas_call(
             functools.partial(kernel, n_img, n_tp),
-            out_shape=jax.ShapeDtypeStruct((rows, out_width), bf16),
+            out_shape=pltpu.VMEM((rows, out_width), bf16),
             in_specs=[pl.BlockSpec(memory_space=pl.ANY)] * 7,
-            out_specs=pl.BlockSpec(memory_space=pl.ANY),
+            out_specs=pl.BlockSpec(memory_space=pltpu.VMEM),
             scratch_shapes=scratch,
             compiler_params=pltpu.CompilerParams(
                 collective_id=0, has_side_effects=True, vmem_limit_bytes=60 * 1024 * 1024),

time: 114 us -> 111 us (0.974)
  local copies, waits for them, and re-layouts: 2.29 us -> 0.97 us
    pallas_call x1, Pallas kernels: 111 us -> 110 us  [on_device(): pl.pallas_call(functools.partial(kernel, n_img, n_tp), out_shape=pltpu.VM...]
    unnamed x1, local copies, waits for them, and re-layouts: 2.29 us -> 0.97 us
where the time goes in v2:
time: 111 us
  Pallas kernels  110 us (99%)
    pallas_call x1, Pallas kernels, on_device(): pl.pallas_call(functools.partial(kernel, n_img, n_tp), out_shape=pltpu.VM...  110 us

profile of v2, /device:TPU:0, one launch (start us, length us, event | category | flops | bytes accessed | tf_op | source)
XLA Modules:
  0.0 110.7 jit_solution(1386979888259439678)
XLA Ops:
  0.0 109.8 %shard_map.73 = bf16[128,4096]{1,0:T(8,128)(2,1)S(1)} custom-call(bf16[128,1024]{1,0:T(8,128)(2,1)} %x_hbm.1, f32[1,1024]{1,0:T(1,128)} %bitcast.5, f32[1,1024]{1,0:T(1,128)} %bitcast.6, bf16[256,1024]{1,0:T(8,128)(2,1)} %up_hbm.1, f32[1,1024]{1,0:T(1,128)} %bitcast.7, bf16[1024,1024]{1,0:T(8,128)(2,1)} %down_hbm.1, f32[1,4096]{1,0:T(1,128)} %bitcast.4), custom_call_target="tpu_custom_call" | custom-call | tf_op jit(solution)/shard_map/pallas_call | solution.py:467
  109.8 1.0 copy.9

commit v3 on v2

--- a/solution.py
+++ b/solution.py
@@ -12,6 +12,7 @@
 UP_STAGES = 2
 LAG = 2
 TILE = 256
+TAIL = 3
 
 
 def portion(size, num, den):
@@ -21,7 +22,7 @@
 def kernel(n_img, n_tp, x_hbm, gain_hbm, nbias_hbm, up_hbm, ubias_hbm, down_hbm, dbias_hbm, out_ref,
            xv, gain, nbias, ubias, dbias, tok, normed, upf, ubf, hidden, dn, pb, from_low, from_high,
            in_sem, own_sem, tu_s, tu_r, td_s, td_r, bs_s, bs_r,
-           dx_s, dx_r, dm_s, dm_r, r1_s, r1_r, r2_s, r2_r, p_s, p_r, lo_s, lo_r, hi_s, hi_r):
+           dx_s, dx_r, dm_s, dm_r, r1_s, r1_r, r2_s, r2_r, p_s, p_r, lo_s, lo_r, hi_s, hi_r, end_r):
     cores = 2 if n_img % 2 == 0 else 1
     pair = 2 if n_tp % 2 == 0 else 1
     n_x, n_g = n_img // cores, n_tp // pair
@@ -35,8 +36,10 @@
     stages = UP_STAGES + n_chunk
     wide = cores * LANES
     n_v = n_chunk * n_x
+    v_last, v_tail = n_v - 1, n_v - TAIL
     xs, ms, hops = range(1, n_x), range(1, pair), range(1, n_g)
-    low_part = portion(u_rows, 3, 8), portion(units, 17, 32)
+    n_tile = units // TILE
+    low_part = portion(u_rows, 1, 4), portion(units, 9, 16)
 
     def at_x(k):
         return {"img": lax.rem(x + k, n_x) * cores + c, "tp": tp}
@@ -91,14 +94,21 @@
     def across(s, kx, km, ref):
         return copy(ref, ref, p_s.at[kind(s)], p_r.at[s, km if is_up(s) else kx], partner)
 
-    def issue(s):
+    def issue_m(s):
         ref = block(s, 0, 0, c)
         for k in ms:
             direct_m(s, k, ref).start()
-        for k in xs:
-            direct_x(s, k, ref).start()
         if cores > 1:
             across(s, 0, 0, ref).start()
+
+    def issue_x(s):
+        ref = block(s, 0, 0, c)
+        for k in xs:
+            direct_x(s, k, ref).start()
+
+    def issue(s):
+        issue_m(s)
+        issue_x(s)
 
     def forward_m(s):
         for km in ms:
@@ -120,10 +130,11 @@
 
     def collect(s, k):
         for km in ms:
-            relay_m(s, k, km, block(s, k, km, c, 0)).wait_recv()
-            relay_x(s, k, km, block(s, k, km, c, 1)).wait_recv()
-            if cores > 1:
-                across(s, k, km, block(s, k, km, c)).start()
+            for part, relay in enumerate((relay_m, relay_x)):
+                ref = block(s, k, km, c, part)
+                relay(s, k, km, ref).wait_recv()
+                if cores > 1:
+                    across(s, k, km, ref).start()
 
     def take_up(s, km):
         if cores > 1:
@@ -184,11 +195,19 @@
     def bias(k, src, slot):
         return copy(src, ubf.at[slot], bs_s.at[slot], bs_r.at[slot], at_m(k))
 
-    def upward(v, d):
-        return copy(pb.at[v, d], from_low.at[v, d], lo_s.at[d - 1], lo_r.at[v, d - 1], at_g(1))
-
-    def downward(v, d):
-        return copy(pb.at[v, d], from_high.at[v, d], hi_s.at[d], hi_r.at[v, d], at_g(n_g - 1))
+    def upward(v, e):
+        part = pl.ds(e + 1, n_g - 1 - e)
+        return copy(pb.at[v, part], from_low.at[v, part], lo_s.at[0], lo_r.at[v], at_g(1))
+
+    def downward(v, e):
+        part = pl.ds(0, n_g - 1 - e)
+        return copy(pb.at[v, part], from_high.at[v, part], hi_s.at[0], hi_r.at[v], at_g(n_g - 1))
+
+    def piece_up(v, d):
+        return copy(pb.at[v, d], from_low.at[v, d], lo_s.at[0], end_r.at[0, v - v_tail, d], at_g(1))
+
+    def piece_down(v, d):
+        return copy(pb.at[v, d], from_high.at[v, d], hi_s.at[0], end_r.at[1, v - v_tail, d], at_g(n_g - 1))
 
     def normalize(values, at):
         values = values.astype(jnp.float32)
@@ -238,7 +257,7 @@
         bias(k, ubias, k - 1).start()
     loads[5].wait()
 
-    def up_rows(km):
+    def up_rows(km, first, last):
         place = lax.rem(m - km + pair, pair)
         biases = ubias if km == 0 else ubf.at[km - 1]
 
@@ -249,7 +268,7 @@
             hidden[:, at] = jax.nn.gelu(summed + biases[:, cols]).astype(jnp.bfloat16)
             return carry
 
-        lax.fori_loop(0, units // TILE, up_tile, 0)
+        lax.fori_loop(first, last, up_tile, 0)
 
     for s in range(max(UP_STAGES, n_g - 1)):
         if 0 < s + 1 < n_g - 1:
@@ -257,16 +276,18 @@
         if s < UP_STAGES:
             forward_m(s)
             forward_x(s)
-    for j in range(min(2, n_chunk)):
-        own_down(j).wait()
-        issue(UP_STAGES + j)
+    own_down(0).wait()
+    issue(UP_STAGES)
+    if n_chunk > 1:
+        own_down(1).wait()
+        issue_m(UP_STAGES + 1)
     token_end()
     for k in hops:
         o = lax.rem(g + k, n_g)
         normalize(tok[o], o)
     for s in range(UP_STAGES):
         take_up(s, 0)
-    up_rows(0)
+    up_rows(0, 0, n_tile)
     for s in range(UP_STAGES):
         for k in xs:
             collect(s, k)
@@ -274,53 +295,92 @@
         bias(km, ubias, km - 1).wait_recv()
         for s in range(UP_STAGES):
             take_up(s, km)
-        up_rows(km)
+        up_rows(km, 0, n_tile // 2)
+        if km == pair - 1:
+            forward_m(UP_STAGES)
+            if n_chunk > 1:
+                issue_x(UP_STAGES + 1)
+        up_rows(km, n_tile // 2, n_tile)
+    if pair == 1 and n_chunk > 1:
+        issue_x(UP_STAGES + 1)
 
     def multiply(v, j, k):
         value = jnp.dot(hidden[...], dn[j * n_x + x_from(k)], preferred_element_type=jnp.float32)
         pb[v] = value.reshape(n_g, rows, wide).astype(jnp.bfloat16)
 
+    upper = 2 * g // n_g
+    far_d = (1 - upper) * (n_g - 1)
+
+    def multiply_far(v, j, k):
+        lines = hidden[pl.ds(pl.multiple_of(far_d * rows, rows), rows), :]
+        value = jnp.dot(lines, dn[j * n_x + x_from(k)], preferred_element_type=jnp.float32)
+        pb[v, far_d] = value.astype(jnp.bfloat16)
+
+    def multiply_rest(v, j, k):
+        if n_g > 1:
+            lines = hidden[pl.ds(pl.multiple_of(upper * rows, rows), (n_g - 1) * rows), :]
+            value = jnp.dot(lines, dn[j * n_x + x_from(k)], preferred_element_type=jnp.float32)
+            pb[v, pl.ds(upper, n_g - 1)] = value.reshape(n_g - 1, rows, wide).astype(jnp.bfloat16)
+
+    def add(v, part, arrived):
+        pb[v, part] = (pb[v, part].astype(jnp.float32) + arrived[v, part].astype(jnp.float32)).astype(jnp.bfloat16)
+
     def pass_on(step):
-        v_up, v_down = step - LAG * g, step - LAG * (n_g - 1 - g)
-        go_up = (g < n_g - 1) & (v_up >= 0) & (v_up < n_v)
-        go_down = (g > 0) & (v_down >= 0) & (v_down < n_v)
-
-        def accumulate(v, d, copies, arrived):
-            copies(v, d).wait_recv()
-            pb[v, d] = (pb[v, d].astype(jnp.float32) + arrived[v, d].astype(jnp.float32)).astype(jnp.bfloat16)
-
-        for k in range(n_g - 1):
-            high, low = n_g - 1 - k, k
-
-            @pl.when(go_up & (g > 0) & (g < high))
+        for e in reversed(range(n_g - 1)):
+            v = step - LAG * e
+
+            @pl.when((g == e) & (v >= 0) & (v < v_tail))
             def _():
-                accumulate(v_up, high, upward, from_low)
-
-            @pl.when(go_down & (g < n_g - 1) & (g > low))
+                if e > 0:
+                    upward(v, e - 1).wait_recv()
+                    add(v, pl.ds(e + 1, n_g - 1 - e), from_low)
+                upward(v, e).start()
+
+            @pl.when((g == n_g - 1 - e) & (v >= 0) & (v < v_tail))
             def _():
-                accumulate(v_down, low, downward, from_high)
-
-            @pl.when(go_up & (g < high))
-            def _():
-                upward(v_up, high).start()
-
-            @pl.when(go_down & (g > low))
-            def _():
-                downward(v_down, low).start()
+                if e > 0:
+                    downward(v, e - 1).wait_recv()
+                    add(v, pl.ds(0, n_g - 1 - e), from_high)
+                downward(v, e).start()
+
+    def pass_pieces(step, first, stop):
+        for e in reversed(range(n_g - 1)):
+            v = step - LAG * e
+            for i in range(first, min(stop, n_g - 1 - e)):
+                for here, d, piece, arrived in (
+                        (e, n_g - 1 - i, piece_up, from_low), (n_g - 1 - e, i, piece_down, from_high)):
+                    @pl.when((g == here) & (v >= v_tail) & (v < n_v))
+                    def _():
+                        if e > 0:
+                            piece(v, d).wait_recv()
+                            add(v, d, arrived)
+                        piece(v, d).start()
+
+    def pass_far(step):
+        pass_on(step)
+        pass_pieces(step, 0, 1)
+
+    def pass_near(step):
+        pass_pieces(step, 1, n_g)
 
     def reduce(v):
         some = (v + n_v - 1) // n_v
         i = (v + n_x - 1) // n_x
         k = lax.rem(v + n_x - 1, n_x) * some + i // n_chunk
         j = i - (k + n_x - 1) // n_x
-
-        @pl.when(g > 0)
-        def _():
-            upward(v, g).wait_recv()
-
-        @pl.when(g < n_g - 1)
-        def _():
-            downward(v, g).wait_recv()
+        for d in range(n_g):
+            @pl.when(g == d)
+            def _():
+                if isinstance(v, int) and v >= v_tail:
+                    if d > 0:
+                        piece_up(v, d).wait_recv()
+                    if d < n_g - 1:
+                        piece_down(v, d).wait_recv()
+                elif n_g > 1:
+                    if d == n_g - 1:
+                        upward(v, d - 1).wait_recv()
+                    if d == 0:
+                        downward(v, n_g - 2).wait_recv()
 
         src_x = x_from(k)
         for core in range(cores):
@@ -334,22 +394,36 @@
 
     settle = LAG * (n_g - 1) + 1
 
+    def settled(v):
+        @pl.when(v >= settle)
+        def _():
+            reduce(v - settle)
+
     def unit(v, j, k):
         take(j + UP_STAGES, k)
         multiply(v, j, k)
-        pass_on(v)
-
-        @pl.when(v >= settle)
-        def _():
-            reduce(v - settle)
-
-    def later(i, base):
+        pass_far(v)
+
+        @pl.when(v < n_v - 2)
+        def _():
+            pass_near(v)
+
+        settled(v)
+
+    def last_unit(j, k):
+        take(j + UP_STAGES, k)
+        multiply_far(v_last, j, k)
+        pass_far(v_last)
+        multiply_rest(v_last, j, k)
+        settled(v_last)
+
+    def later(i, base, stop):
         def one(k, carry):
             collect(i + UP_STAGES, k)
             unit(base + k, i, k)
             return carry
 
-        lax.fori_loop(1, n_x, one, 0)
+        lax.fori_loop(1, stop, one, 0)
 
     def start(i):
         @pl.when(i + 2 < n_chunk)
@@ -362,26 +436,44 @@
         unit(n_x * (i - 1) + 1, i, 0)
         forward_x(i + UP_STAGES)
         start(i)
-        later(i - 1, n_x * (i - 1) + 1)
+        later(i - 1, n_x * (i - 1) + 1, n_x)
         return carry
 
-    forward_m(UP_STAGES)
     unit(0, 0, 0)
     forward_x(UP_STAGES)
     start(0)
-    lax.fori_loop(1, n_chunk, tick, 0)
-    later(n_chunk - 1, n_x * (n_chunk - 1))
+    if n_x > 1 and n_chunk > 1:
+        forward_m(1 + UP_STAGES)
+        unit(1, 1, 0)
+        for k in xs:
+            collect(UP_STAGES, k)
+        forward_x(1 + UP_STAGES)
+        start(1)
+        for k in xs:
+            unit(1 + k, 0, k)
+        lax.fori_loop(2, n_chunk, tick, 0)
+        later(n_chunk - 1, n_x * (n_chunk - 1), n_x - 1)
+        collect(n_chunk - 1 + UP_STAGES, n_x - 1)
+        last_unit(n_chunk - 1, n_x - 1)
+    else:
+        lax.fori_loop(1, n_chunk - 1, tick, 0)
+        forward_m(n_chunk - 1 + UP_STAGES)
+        forward_x(n_chunk - 1 + UP_STAGES)
+        last_unit(n_chunk - 1, 0)
 
     def drain(step, carry):
-        pass_on(step)
+        pass_far(step)
+        pass_near(step - 2)
         return carry
 
     def reduce_tick(v, carry):
         reduce(v)
         return carry
 
-    lax.fori_loop(n_v, n_v + LAG * (n_g - 2), drain, 0)
-    lax.fori_loop(max(n_v - settle, 0), n_v, reduce_tick, 0)
+    lax.fori_loop(n_v, n_v + LAG * (n_g - 2) + 2, drain, 0)
+    lax.fori_loop(max(n_v - settle, 0), v_tail, reduce_tick, 0)
+    for v in range(v_tail, n_v):
+        reduce(v)
 
     for t in range(2):
         s = 0 if t == 0 else UP_STAGES
@@ -404,16 +496,16 @@
         if cores > 1:
             ref = upf.at[:, pl.ds(0, n_x * depth), :] if t == 0 else dn.at[:, :, pl.ds(0, LANES)]
             across(s, 0, 0, ref).wait_send()
-    for d in range(n_g):
-        @pl.when(g < d)
-        def _():
-            ref = pb.at[:, d]
-            copy(ref, ref, lo_s.at[d - 1], lo_r.at[0, 0], at_g(1)).wait_send()
-
-        @pl.when(g > d)
-        def _():
-            ref = pb.at[:, d]
-            copy(ref, ref, hi_s.at[d], hi_r.at[0, 0], at_g(n_g - 1)).wait_send()
+    for e in range(n_g - 1):
+        @pl.when(g == e)
+        def _():
+            ref = pb.at[:, pl.ds(e + 1, n_g - 1 - e)]
+            copy(ref, ref, lo_s.at[0], lo_r.at[0], at_g(1)).wait_send()
+
+        @pl.when(g == n_g - 1 - e)
+        def _():
+            ref = pb.at[:, pl.ds(0, n_g - 1 - e)]
+            copy(ref, ref, hi_s.at[0], hi_r.at[0], at_g(n_g - 1)).wait_send()
     for e in range(n_g - 1):
         @pl.when((g >= e) & (g < n_g - 1))
         def _():
@@ -463,7 +555,7 @@
         scratch += [dma((2, ox)), dma((stages, ox)), dma((2, om)), dma((stages, om))]
         scratch += [dma((2, ox, om)), dma((stages, ox, om))] * 2
         scratch += [dma((2,)), dma((stages, max(n_x, pair)))]
-        scratch += [dma((og,)), dma((n_v, og))] * 2
+        scratch += [dma((1,)), dma((n_v,))] * 2 + [dma((2, TAIL, n_g))]
         return pl.pallas_call(
             functools.partial(kernel, n_img, n_tp),
             out_shape=pltpu.VMEM((rows, out_width), bf16),

time: 111 us -> 110 us (level)
    pallas_call x1, Pallas kernels: 110 us -> 109 us  [on_device(): pl.pallas_call(functools.partial(kernel, n_img, n_tp), out_shape=pltpu.VM...]
where the time goes in v3:
time: 110 us
  Pallas kernels  109 us (99%)
    pallas_call x1, Pallas kernels, on_device(): pl.pallas_call(functools.partial(kernel, n_img, n_tp), out_shape=pltpu.VM...  109 us

profile of v3, /device:TPU:0, one launch (start us, length us, event | category | flops | bytes accessed | tf_op | source)
XLA Modules:
  0.0 109.6 jit_solution(13436345602286935936)
XLA Ops:
  0.0 108.6 %shard_map.73 = bf16[128,4096]{1,0:T(8,128)(2,1)S(1)} custom-call(bf16[128,1024]{1,0:T(8,128)(2,1)} %x_hbm.1, f32[1,1024]{1,0:T(1,128)} %bitcast.5, f32[1,1024]{1,0:T(1,128)} %bitcast.6, bf16[256,1024]{1,0:T(8,128)(2,1)} %up_hbm.1, f32[1,1024]{1,0:T(1,128)} %bitcast.7, bf16[1024,1024]{1,0:T(8,128)(2,1)} %down_hbm.1, f32[1,4096]{1,0:T(1,128)} %bitcast.4), custom_call_target="tpu_custom_call" | custom-call | tf_op jit(solution)/shard_map/pallas_call | solution.py:559
  108.6 1.0 copy.9

commit v4 on v3

--- a/solution.py
+++ b/solution.py
@@ -12,7 +12,7 @@
 UP_STAGES = 2
 LAG = 2
 TILE = 256
-TAIL = 3
+TAIL = 2
 
 
 def portion(size, num, den):
@@ -238,24 +238,24 @@
     own_up = upf.at[m, pl.ds(pl.multiple_of(img * depth, depth), depth), :]
     loads = [pltpu.make_async_copy(a, b, in_sem.at[i]) for i, (a, b) in enumerate((
         (x_hbm, xv), (up_hbm, own_up), (gain_hbm, gain), (nbias_hbm, nbias), (ubias_hbm, ubias), (dbias_hbm, dbias)))]
-    for load in loads:
-        load.start()
+    for i in (1, 0, 2, 3, 4, 5):
+        loads[i].start()
+    loads[1].wait()
+    ends = (g + n_g - 1) // n_g + (2 * n_g - 2 - g) // n_g
+    pl.semaphore_wait(barrier, len(near) + ends)
+
+    for s in range(UP_STAGES):
+        issue(s)
+    loads[0].wait()
+    if n_g > 1:
+        token_start(0)
     for j in range(n_chunk):
         own_down(j).start()
-    for i in (0, 2, 3, 4, 1):
+    for i in (2, 3, 4, 5):
         loads[i].wait()
-    normalize(xv[...], g)
-
-    ends = (g + n_g - 1) // n_g + (2 * n_g - 2 - g) // n_g
-    pl.semaphore_wait(barrier, len(near) + ends)
-
-    for s in range(UP_STAGES):
-        issue(s)
-    if n_g > 1:
-        token_start(0)
     for k in ms:
         bias(k, ubias, k - 1).start()
-    loads[5].wait()
+    normalize(xv[...], g)
 
     def up_rows(km, first, last):
         place = lax.rem(m - km + pair, pair)

time: 110 us -> 109 us (level)
  no operation moved by 1% of the time
where the time goes in v4:
time: 109 us
  Pallas kernels  108 us (99%)
    pallas_call x1, Pallas kernels, on_device(): pl.pallas_call(functools.partial(kernel, n_img, n_tp), out_shape=pltpu.VM...  108 us

profile of v4, /device:TPU:0, one launch (start us, length us, event | category | flops | bytes accessed | tf_op | source)
XLA Modules:
  0.0 109.2 jit_solution(5153400761748792458)
XLA Ops:
  0.0 108.2 %shard_map.73 = bf16[128,4096]{1,0:T(8,128)(2,1)S(1)} custom-call(bf16[128,1024]{1,0:T(8,128)(2,1)} %x_hbm.1, f32[1,1024]{1,0:T(1,128)} %bitcast.5, f32[1,1024]{1,0:T(1,128)} %bitcast.6, bf16[256,1024]{1,0:T(8,128)(2,1)} %up_hbm.1, f32[1,1024]{1,0:T(1,128)} %bitcast.7, bf16[1024,1024]{1,0:T(8,128)(2,1)} %down_hbm.1, f32[1,4096]{1,0:T(1,128)} %bitcast.4), custom_call_target="tpu_custom_call" | custom-call | tf_op jit(solution)/shard_map/pallas_call | solution.py:559
  108.2 1.0 copy.9

commit v5 on v4

--- a/solution.py
+++ b/solution.py
@@ -12,7 +12,7 @@
 UP_STAGES = 2
 LAG = 2
 TILE = 256
-TAIL = 2
+TAIL = 3
 
 
 def portion(size, num, den):
@@ -203,11 +203,21 @@
         part = pl.ds(0, n_g - 1 - e)
         return copy(pb.at[v, part], from_high.at[v, part], hi_s.at[0], hi_r.at[v], at_g(n_g - 1))
 
-    def piece_up(v, d):
-        return copy(pb.at[v, d], from_low.at[v, d], lo_s.at[0], end_r.at[0, v - v_tail, d], at_g(1))
-
-    def piece_down(v, d):
-        return copy(pb.at[v, d], from_high.at[v, d], hi_s.at[0], end_r.at[1, v - v_tail, d], at_g(n_g - 1))
+    def slab(d, h):
+        if h is None:
+            return d
+        return d, pl.ds(h * (rows // 2), rows // 2)
+
+    def piece_up(v, d, h):
+        at = slab(d, h)
+        at = (at,) if h is None else at
+        return copy(pb.at[(v,) + at], from_low.at[(v,) + at], lo_s.at[0], end_r.at[0, v - v_tail, d if h != 1 else n_g], at_g(1))
+
+    def piece_down(v, d, h):
+        at = slab(d, h)
+        at = (at,) if h is None else at
+        return copy(pb.at[(v,) + at], from_high.at[(v,) + at], hi_s.at[0], end_r.at[1, v - v_tail, d if h != 1 else n_g],
+                    at_g(n_g - 1))
 
     def normalize(values, at):
         values = values.astype(jnp.float32)
@@ -323,7 +333,8 @@
             pb[v, pl.ds(upper, n_g - 1)] = value.reshape(n_g - 1, rows, wide).astype(jnp.bfloat16)
 
     def add(v, part, arrived):
-        pb[v, part] = (pb[v, part].astype(jnp.float32) + arrived[v, part].astype(jnp.float32)).astype(jnp.bfloat16)
+        at = (v,) + part if isinstance(part, tuple) else (v, part)
+        pb[at] = (pb[at].astype(jnp.float32) + arrived[at].astype(jnp.float32)).astype(jnp.bfloat16)
 
     def pass_on(step):
         for e in reversed(range(n_g - 1)):
@@ -351,10 +362,11 @@
                         (e, n_g - 1 - i, piece_up, from_low), (n_g - 1 - e, i, piece_down, from_high)):
                     @pl.when((g == here) & (v >= v_tail) & (v < n_v))
                     def _():
-                        if e > 0:
-                            piece(v, d).wait_recv()
-                            add(v, d, arrived)
-                        piece(v, d).start()
+                        for h in (0, 1) if i == 0 else (None,):
+                            if e > 0:
+                                piece(v, d, h).wait_recv()
+                                add(v, slab(d, h), arrived)
+                            piece(v, d, h).start()
 
     def pass_far(step):
         pass_on(step)
@@ -373,9 +385,11 @@
             def _():
                 if isinstance(v, int) and v >= v_tail:
                     if d > 0:
-                        piece_up(v, d).wait_recv()
+                        for h in (0, 1) if d == n_g - 1 else (None,):
+                            piece_up(v, d, h).wait_recv()
                     if d < n_g - 1:
-                        piece_down(v, d).wait_recv()
+                        for h in (0, 1) if d == 0 else (None,):
+                            piece_down(v, d, h).wait_recv()
                 elif n_g > 1:
                     if d == n_g - 1:
                         upward(v, d - 1).wait_recv()
@@ -555,7 +569,7 @@
         scratch += [dma((2, ox)), dma((stages, ox)), dma((2, om)), dma((stages, om))]
         scratch += [dma((2, ox, om)), dma((stages, ox, om))] * 2
         scratch += [dma((2,)), dma((stages, max(n_x, pair)))]
-        scratch += [dma((1,)), dma((n_v,))] * 2 + [dma((2, TAIL, n_g))]
+        scratch += [dma((1,)), dma((n_v,))] * 2 + [dma((2, TAIL, n_g + 1))]
         return pl.pallas_call(
             functools.partial(kernel, n_img, n_tp),
             out_shape=pltpu.VMEM((rows, out_width), bf16),

time: 109 us -> 108 us (level)
  no operation moved by 1% of the time
where the time goes in v5:
time: 108 us
  Pallas kernels  107 us (99%)
    pallas_call x1, Pallas kernels, on_device(): pl.pallas_call(functools.partial(kernel, n_img, n_tp), out_shape=pltpu.VM...  107 us

profile of v5, /device:TPU:0, one launch (start us, length us, event | category | flops | bytes accessed | tf_op | source)
XLA Modules:
  0.0 108.3 jit_solution(281695220633788384)
XLA Ops:
  0.0 107.3 %shard_map.73 = bf16[128,4096]{1,0:T(8,128)(2,1)S(1)} custom-call(bf16[128,1024]{1,0:T(8,128)(2,1)} %x_hbm.1, f32[1,1024]{1,0:T(1,128)} %bitcast.5, f32[1,1024]{1,0:T(1,128)} %bitcast.6, bf16[256,1024]{1,0:T(8,128)(2,1)} %up_hbm.1, f32[1,1024]{1,0:T(1,128)} %bitcast.7, bf16[1024,1024]{1,0:T(8,128)(2,1)} %down_hbm.1, f32[1,4096]{1,0:T(1,128)} %bitcast.4), custom_call_target="tpu_custom_call" | custom-call | tf_op jit(solution)/shard_map/pallas_call | solution.py:573
  107.3 1.0 copy.9

commit v6 on v5

--- a/solution.py
+++ b/solution.py
@@ -39,7 +39,7 @@
     v_last, v_tail = n_v - 1, n_v - TAIL
     xs, ms, hops = range(1, n_x), range(1, pair), range(1, n_g)
     n_tile = units // TILE
-    low_part = portion(u_rows, 1, 4), portion(units, 9, 16)
+    low_part = portion(u_rows, 3, 8), portion(units, 17, 32)
 
     def at_x(k):
         return {"img": lax.rem(x + k, n_x) * cores + c, "tp": tp}
@@ -447,9 +447,9 @@
 
     def tick(i, carry):
         forward_m(i + UP_STAGES)
-        unit(n_x * (i - 1) + 1, i, 0)
         forward_x(i + UP_STAGES)
         start(i)
+        unit(n_x * (i - 1) + 1, i, 0)
         later(i - 1, n_x * (i - 1) + 1, n_x)
         return carry
 
@@ -569,7 +569,7 @@
         scratch += [dma((2, ox)), dma((stages, ox)), dma((2, om)), dma((stages, om))]
         scratch += [dma((2, ox, om)), dma((stages, ox, om))] * 2
         scratch += [dma((2,)), dma((stages, max(n_x, pair)))]
-        scratch += [dma((1,)), dma((n_v,))] * 2 + [dma((2, TAIL, n_g + 1))]
+        scratch += [dma((1,)), dma((max(n_v - TAIL, 1),))] * 2 + [dma((2, TAIL, n_g + 1))]
         return pl.pallas_call(
             functools.partial(kernel, n_img, n_tp),
             out_shape=pltpu.VMEM((rows, out_width), bf16),

time: 108 us -> 107 us (level)
  Pallas kernels: 107 us -> 105 us
    pallas_call x1, Pallas kernels: 107 us -> 105 us  [on_device(): pl.pallas_call(functools.partial(kernel, n_img, n_tp), out_shape=pltpu.VM...]
where the time goes in v6:
time: 107 us; the launch traced here: 106 us
  Pallas kernels  105 us (98%)
    pallas_call x1, Pallas kernels, on_device(): pl.pallas_call(functools.partial(kernel, n_img, n_tp), out_shape=pltpu.VM...  105 us

profile of v6, /device:TPU:0, one launch (start us, length us, event | category | flops | bytes accessed | tf_op | source)
XLA Modules:
  0.0 106.5 jit_solution(6689790534306294444)
XLA Ops:
  0.0 105.5 %shard_map.73 = bf16[128,4096]{1,0:T(8,128)(2,1)S(1)} custom-call(bf16[128,1024]{1,0:T(8,128)(2,1)} %x_hbm.1, f32[1,1024]{1,0:T(1,128)} %bitcast.5, f32[1,1024]{1,0:T(1,128)} %bitcast.6, bf16[256,1024]{1,0:T(8,128)(2,1)} %up_hbm.1, f32[1,1024]{1,0:T(1,128)} %bitcast.7, bf16[1024,1024]{1,0:T(8,128)(2,1)} %down_hbm.1, f32[1,4096]{1,0:T(1,128)} %bitcast.4), custom_call_target="tpu_custom_call" | custom-call | tf_op jit(solution)/shard_map/pallas_call | solution.py:573
  105.5 1.0 copy.9

commit v7 on v6

--- a/solution.py
+++ b/solution.py
@@ -114,10 +114,10 @@
         for km in ms:
             ref = block(s, 0, km, c)
             direct_m(s, km, ref).wait_recv()
+            for k in xs:
+                relay_x(s, k, km, block(s, 0, km, c, 1)).start()
             if cores > 1:
                 across(s, 0, km, ref).start()
-            for k in xs:
-                relay_x(s, k, km, block(s, 0, km, c, 1)).start()
 
     def forward_x(s):
         for k in xs:

time: 107 us -> 107 us (level)
  no operation moved by 1% of the time
where the time goes in v7:
time: 107 us; the launch traced here: 106 us
  Pallas kernels  105 us (98%)
    pallas_call x1, Pallas kernels, on_device(): pl.pallas_call(functools.partial(kernel, n_img, n_tp), out_shape=pltpu.VM...  105 us

profile of v7, /device:TPU:0, one launch (start us, length us, event | category | flops | bytes accessed | tf_op | source)
XLA Modules:
  0.0 106.5 jit_solution(1851246279290232136)
XLA Ops:
  0.0 105.5 %shard_map.73 = bf16[128,4096]{1,0:T(8,128)(2,1)S(1)} custom-call(bf16[128,1024]{1,0:T(8,128)(2,1)} %x_hbm.1, f32[1,1024]{1,0:T(1,128)} %bitcast.5, f32[1,1024]{1,0:T(1,128)} %bitcast.6, bf16[256,1024]{1,0:T(8,128)(2,1)} %up_hbm.1, f32[1,1024]{1,0:T(1,128)} %bitcast.7, bf16[1024,1024]{1,0:T(8,128)(2,1)} %down_hbm.1, f32[1,4096]{1,0:T(1,128)} %bitcast.4), custom_call_target="tpu_custom_call" | custom-call | tf_op jit(solution)/shard_map/pallas_call | solution.py:573
  105.5 1.0 copy.9
